TPU v7x, 32 devices: a whole 2x2x4 slice. The times are simulated.
32 devices in a mesh: tm: 8 (over z, x), env: 4 (over y, core).
Axes of the slice: x: 2, y: 2, z: 4, core: 2. Of those that a mesh axis runs over, the one named last changes fastest.
Arguments:
- init_state: float32 [70, 1024], P(None, 'env'), may hold values from -6 to 6
- torque: float32 [32, 35, 1024], P('tm', None, 'env'), may hold values from -192 to 192
- contact: int32 [32, 1024], P('tm', 'env'), may hold values 0 or 1
- mass_inverse: float32 [16, 35, 35], P('tm'), may hold values from -0.014 to 1.5, as said below
- stiffness: float32 [35], replicated, may hold values from 10 to 100
- damping: float32 [35], replicated, may hold values from 0.5 to 5
- gravity: float32 [35], replicated, may hold values from 1 to 10
- contact_stiffness: float32 [35], replicated, may hold values from 20 to 100
- contact_damping: float32 [35], replicated, may hold values from 0.5 to 3
Outputs:
- final_states: float32 [16, 70, 1024], P('tm', None, 'env')
- corrections: float32 [3, 1024], P(None, 'env')
Inputs may be any that keep to these rules, and one draw needn't show every extreme that they name: `mass_inverse`: each matrix is symmetric, and each diagonal entry exceeds the sum of the magnitudes of the other entries of its row.
All inputs are finite; a program needn't handle non-finite values. No bound on the sum of `contact` on one device may be relied on, other than what follows from the above.
Results may differ from a plain program's by a relative error of at most 0.00025.
Values sent between devices are 32-bit elements; how exact they have to be, the bound alone decides.
A program may use at most 64 MiB of HBM per device.

v0:
```python
import jax
import jax.numpy as jnp
from jax import lax
from jax.sharding import PartitionSpec as P

DOF = 35
HS = 2
SUB = 32
ITERS = 3
step_length = 0.05


def exact_dot(left, right):
    return jnp.dot(left, right, precision=lax.Precision.HIGHEST, preferred_element_type=jnp.float32)


def coarse_one(state_now, torque_steps, mean_steps, inverse, params):
    stiffness, damping, gravity, contact_stiffness, contact_damping = params
    joint_pos = state_now[:DOF]
    joint_vel = state_now[DOF:]
    for step_pos in range(HS):
        spring = (stiffness + gravity + mean_steps[step_pos] * contact_stiffness)[:, None]
        friction = (damping + mean_steps[step_pos] * contact_damping)[:, None]
        force = torque_steps[step_pos] - spring * joint_pos - friction * joint_vel
        joint_vel = joint_vel + step_length * exact_dot(inverse, force)
        joint_pos = joint_pos + step_length * joint_vel
    return jnp.concatenate([joint_pos, joint_vel], axis=0)


def fine_one(state_now, torque_steps, contact_steps, inverse, params):
    stiffness, damping, gravity, contact_stiffness, contact_damping = params
    fine_dt = step_length / SUB
    joint_pair = (state_now[:DOF], state_now[DOF:])
    for step_pos in range(HS):
        torque_here = torque_steps[step_pos]
        contact_here = contact_steps[step_pos][None, :]

        def substep(counter, pair_now):
            joint_pos, joint_vel = pair_now
            force = (
                torque_here
                - stiffness[:, None] * joint_pos
                - damping[:, None] * joint_vel
                - gravity[:, None] * jnp.sin(joint_pos)
                - contact_here
                * (contact_stiffness[:, None] * joint_pos + contact_damping[:, None] * joint_vel)
            )
            joint_vel = joint_vel + fine_dt * exact_dot(inverse, force)
            joint_pos = joint_pos + fine_dt * joint_vel
            return (joint_pos, joint_vel)

        joint_pair = lax.fori_loop(0, SUB, substep, joint_pair, unroll=min(8, SUB))
    return jnp.concatenate([joint_pair[0], joint_pair[1]], axis=0)


def body(
    init_state,
    torque,
    contact,
    mass_inverse,
    stiffness,
    damping,
    gravity,
    contact_stiffness,
    contact_damping,
):
    params = (stiffness, damping, gravity, contact_stiffness, contact_damping)
    local_slices = mass_inverse.shape[0]
    env_local = init_state.shape[1]
    state_rows = init_state.shape[0]
    torque_steps = torque.reshape(local_slices, HS, DOF, env_local)
    contact_float = contact.astype(jnp.float32)
    contact_steps = contact_float.reshape(local_slices, HS, env_local)
    totals = lax.psum(jnp.sum(contact_float, axis=1), "env")
    mean_steps = (totals / (env_local * lax.axis_size("env"))).reshape(local_slices, HS)
    eye_state = jnp.eye(state_rows, dtype=jnp.float32)
    zero_shift = jnp.zeros((state_rows, env_local), jnp.float32)
    no_force = jnp.zeros((local_slices, HS, DOF, 1), jnp.float32)
    step_maps = jax.vmap(coarse_one, in_axes=(None, 0, 0, 0, None))(
        eye_state, no_force, mean_steps, mass_inverse, params
    )
    coarse_free = jax.vmap(coarse_one, in_axes=(0, 0, 0, 0, None))(
        jnp.zeros((local_slices, state_rows, env_local), jnp.float32),
        torque_steps,
        mean_steps,
        mass_inverse,
        params,
    )
    device_map = eye_state
    for slot_pos in range(local_slices):
        device_map = exact_dot(step_maps[slot_pos], device_map)
    all_maps = lax.all_gather(device_map[None], "tm", axis=0, tiled=True)
    my_index = lax.axis_index("tm")

    def backward(product, inputs):
        position, this_map = inputs
        active = position < my_index
        emitted = jnp.where(active, product, 0.0)
        following = jnp.where(active, exact_dot(product, this_map), eye_state)
        return (following, emitted)

    positions = jnp.arange(lax.axis_size("tm"), dtype=jnp.int32)
    lead_map, phi_rows = lax.scan(backward, eye_state, (positions, all_maps), reverse=True)
    lead_state = exact_dot(lead_map, init_state)

    def sweep(offsets):
        local_shift = zero_shift
        for slot_pos in range(local_slices):
            local_shift = exact_dot(step_maps[slot_pos], local_shift) + offsets[slot_pos]
        entry = lead_state + jnp.einsum(
            "mij,mje->ie",
            phi_rows,
            lax.all_gather(local_shift[None], "tm", axis=0, tiled=True),
            precision=lax.Precision.HIGHEST,
        )
        start_list = []
        end_list = []
        current = entry
        for slot_pos in range(local_slices):
            start_list.append(current)
            current = exact_dot(step_maps[slot_pos], current) + offsets[slot_pos]
            end_list.append(current)
        return (jnp.stack(start_list), jnp.stack(end_list))

    starts, ends = sweep(coarse_free)
    fine_all = jax.vmap(fine_one, in_axes=(0, 0, 0, 0, None))
    records = []
    for iteration in range(ITERS):
        fine_end = fine_all(starts, torque_steps, contact_steps, mass_inverse, params)
        jumps = fine_end - jnp.einsum(
            "sij,sje->sie", step_maps, starts, precision=lax.Precision.HIGHEST
        )
        new_starts, new_ends = sweep(jumps)
        local_max = jnp.max(jnp.sqrt(jnp.sum((new_ends - ends) ** 2, axis=1)), axis=0)
        records.append(lax.pmax(local_max, "tm"))
        starts, ends = (new_starts, new_ends)
    corrections = jnp.stack(records)
    return (ends, corrections)


def solution(mesh):
    placed = (
        P(None, "env"),
        P("tm", None, "env"),
        P("tm", "env"),
        P("tm", None, None),
        P(),
        P(),
        P(),
        P(),
        P(),
    )
    return jax.shard_map(
        body,
        mesh=mesh,
        in_specs=placed,
        out_specs=(P("tm", None, "env"), P(None, "env")),
        check_vma=False,
    )
```

profile of v0, /device:TPU:0, one launch (start us, length us, event | category | flops | bytes accessed | tf_op | source)
XLA Modules:
  0.0 318.0 jit_solution(16330962543061578949)
XLA Ops:
  0.6 0.8 convert_reduce_fusion
  1.5 8.4 %psum.7 = f32[4]{0:T(128)S(1)} all-reduce(f32[4]{0:T(128)S(1)} %convert_reduce_fusion), channel_id=1, replica_groups=mesh['tm'=8,'env'=4] {'env'}, use_global_device_ids=true, to_apply=%region_1.0 | all-reduce | flops 4 | bytes 32 | tf_op jit(solution)/shard_map/psum | solution.py:74
  10.2 0.6 copy-done.4
  10.8 0.6 copy-done.1
  11.8 0.7 copy-done.6
  13.6 31.3 %all-gather.5 = f32[8,70,70]{2,1,0:T(8,128)S(1)} all-gather(f32[1,70,70]{2,1,0:T(8,128)S(1)} %convolution_bitcast_fusion.5), channel_id=2, replica_groups=mesh['tm'=8,'env'=4] {'tm'}, dimensions={0}, use_global_device_ids=true | all-gather | bytes 176400 | tf_op jit(solution)/shard_map/all_gather | solution.py:92
  44.9 12.7 %while.95 = (s32[]{:T(128)}, f32[70,70]{0,1:T(8,128)S(1)}, f32[8,70,70]{1,2,0:T(8,128)S(1)}, s32[8]{0:T(128)S(1)}, s32[]{:T(128)}, /*index=5*/f32[8,70,70]{2,1,0:T(8,128)S(1)}, s32[]{:T(128)}, s32[]{:T(128)}) while((s32[]{:T(128)}, f32[70,70]{0,1:T(8,128)S(1)}, f32[8,70,70]{1,2,0:T(8,128)S(1)}, s32[8]{0:T(128)S(1)}, s32[]{:T(128)}, ...), condition=%wide.region_3.4_spmd.clone, body=%wide.region_2.3_spmd.clone.sunk | while | flops 4135604 | bytes 206392 | solution.py:103
  44.9 0.6 dynamic_slice.29
  46.5 0.6 dynamic_slice.29
  48.1 0.6 dynamic_slice.29
  49.7 0.6 dynamic_slice.29
  51.2 0.6 dynamic_slice.29
  52.8 0.6 dynamic_slice.29
  54.4 0.6 dynamic_slice.29
  56.0 0.6 dynamic_slice.29
  59.6 31.5 %all-gather.6 = f32[8,70,256]{2,1,0:T(8,128)S(1)} all-gather(f32[1,70,256]{2,1,0:T(8,128)S(1)} %fusion.1027), channel_id=3, replica_groups=mesh['tm'=8,'env'=4] {'tm'}, dimensions={0}, use_global_device_ids=true | all-gather | bytes 645120 | tf_op jit(solution)/shard_map/all_gather | solution.py:113
  91.1 0.7 fusion.1026
  92.3 0.7 copy-done.8
  93.1 17.1 %while.89 = (s32[]{:T(128)}, f32[2,35,256]{2,1,0:T(8,128)S(1)}, f32[2,35,256]{2,1,0:T(8,128)S(1)}, f32[35]{0:T(128)S(1)}, f32[2,35,256]{2,1,0:T(8,128)S(1)}, /*i...) while((s32[]{:T(128)}, f32[2,35,256]{2,1,0:T(8,128)S(1)}, ...), condition=%wide.region_5.6_spmd, body=%wide.region_4.5_spmd.sunk | while | flops 62504960 | bytes 2680981 | solution.py:52
  93.6 0.5 multiply_add_fusion.107
  96.8 0.5 multiply_add_fusion.110
  97.9 0.5 multiply_add_fusion.107
  110.2 17.2 %while.90 = (s32[]{:T(128)}, f32[2,35,256]{2,1,0:T(8,128)S(1)}, f32[2,35,256]{2,1,0:T(8,128)S(1)}, f32[35]{0:T(128)S(1)}, f32[2,35,256]{2,1,0:T(8,128)S(1)}, /*i...) while((s32[]{:T(128)}, f32[2,35,256]{2,1,0:T(8,128)S(1)}, ...), condition=%wide.region_7.8_spmd, body=%wide.region_6.7_spmd.sunk | while | flops 62504960 | bytes 2680981 | solution.py:52
  110.8 0.5 multiply_add_fusion.111
  111.8 0.5 multiply_add_fusion.112
  114.0 0.5 multiply_add_fusion.114
  115.1 0.5 multiply_add_fusion.111
  116.1 0.5 multiply_add_fusion.112
  119.4 0.5 multiply_add_fusion.111
  120.4 0.5 multiply_add_fusion.112
  122.6 0.5 multiply_add_fusion.114
  123.6 0.5 multiply_add_fusion.111
  124.7 0.5 multiply_add_fusion.112
  126.9 0.5 multiply_add_fusion.114
  127.9 31.5 %all-gather.7 = f32[8,70,256]{2,1,0:T(8,128)S(1)} all-gather(f32[1,70,256]{2,1,0:T(8,128)S(1)} %fusion.1025), channel_id=4, replica_groups=mesh['tm'=8,'env'=4] {'tm'}, dimensions={0}, use_global_device_ids=true | all-gather | bytes 645120 | tf_op jit(solution)/shard_map/all_gather | solution.py:113
  159.4 0.7 fusion.1024
  160.5 17.2 %while.91 = (s32[]{:T(128)}, f32[2,35,256]{2,1,0:T(8,128)S(1)}, f32[2,35,256]{2,1,0:T(8,128)S(1)}, f32[35]{0:T(128)S(1)}, f32[2,35,256]{2,1,0:T(8,128)S(1)}, /*i...) while((s32[]{:T(128)}, f32[2,35,256]{2,1,0:T(8,128)S(1)}, ...), condition=%wide.region_9.10_spmd, body=%wide.region_8.9_spmd.sunk | while | flops 62504960 | bytes 2680981 | solution.py:52
  177.7 17.2 %while.92 = (s32[]{:T(128)}, f32[2,35,256]{2,1,0:T(8,128)S(1)}, f32[2,35,256]{2,1,0:T(8,128)S(1)}, f32[35]{0:T(128)S(1)}, f32[2,35,256]{2,1,0:T(8,128)S(1)}, /*i...) while((s32[]{:T(128)}, f32[2,35,256]{2,1,0:T(8,128)S(1)}, ...), condition=%wide.region_11.12_spmd, body=%wide.region_10.11_spmd.sunk | while | flops 62504960 | bytes 2680981 | solution.py:52
  178.2 0.5 multiply_add_fusion.119
  179.3 0.5 multiply_add_fusion.120
  182.5 0.5 multiply_add_fusion.119
  183.6 0.5 multiply_add_fusion.120
  186.8 0.5 multiply_add_fusion.119
  187.9 0.5 multiply_add_fusion.120
  191.1 0.5 multiply_add_fusion.119
  192.2 0.5 multiply_add_fusion.120
  194.3 0.5 multiply_add_fusion.122
  195.3 31.5 %all-gather.8 = f32[8,70,256]{2,1,0:T(8,128)S(1)} all-gather(f32[1,70,256]{2,1,0:T(8,128)S(1)} %fusion.1023), channel_id=5, replica_groups=mesh['tm'=8,'env'=4] {'tm'}, dimensions={0}, use_global_device_ids=true | all-gather | bytes 645120 | tf_op jit(solution)/shard_map/all_gather | solution.py:113
  226.9 0.7 fusion.1022
  228.0 17.2 %while.93 = (s32[]{:T(128)}, f32[2,35,256]{2,1,0:T(8,128)S(1)}, f32[2,35,256]{2,1,0:T(8,128)S(1)}, f32[35]{0:T(128)S(1)}, f32[2,35,256]{2,1,0:T(8,128)S(1)}, /*i...) while((s32[]{:T(128)}, f32[2,35,256]{2,1,0:T(8,128)S(1)}, ...), condition=%wide.region_13.14_spmd, body=%wide.region_12.13_spmd.sunk | while | flops 62504960 | bytes 2680981 | solution.py:52
  245.1 17.2 %while.94 = (s32[]{:T(128)}, f32[2,35,256]{2,1,0:T(8,128)S(1)}, f32[2,35,256]{2,1,0:T(8,128)S(1)}, f32[35]{0:T(128)S(1)}, f32[2,35,256]{2,1,0:T(8,128)S(1)}, /*i...) while((s32[]{:T(128)}, f32[2,35,256]{2,1,0:T(8,128)S(1)}, ...), condition=%wide.region_15.16_spmd, body=%wide.region_14.15_spmd.sunk | while | flops 62504960 | bytes 2680981 | solution.py:52
  245.7 0.5 multiply_add_fusion.127
  248.9 0.5 multiply_add_fusion.130
  250.0 0.5 multiply_add_fusion.127
  253.2 0.5 multiply_add_fusion.130
  254.3 0.5 multiply_add_fusion.127
  257.5 0.5 multiply_add_fusion.130
  258.6 0.5 multiply_add_fusion.127
  261.8 0.5 multiply_add_fusion.130
  262.8 31.3 %all-gather.9 = f32[8,70,256]{2,1,0:T(8,128)S(1)} all-gather(f32[1,70,256]{2,1,0:T(8,128)S(1)} %fusion.1021), channel_id=6, replica_groups=mesh['tm'=8,'env'=4] {'tm'}, dimensions={0}, use_global_device_ids=true | all-gather | bytes 645120 | tf_op jit(solution)/shard_map/all_gather | solution.py:113
  294.2 0.7 fusion.1020
  295.3 0.7 copy.115
  296.1 21.2 %all-reduce = (f32[1,256]{1,0:T(1,128)S(1)}, f32[1,256]{1,0:T(1,128)S(1)}, f32[1,256]{1,0:T(1,128)S(1)}) all-reduce(f32[1,256]{1,0:T(1,128)S(1)} %bitcast.663, f32[1,256]{1,0:T(1,128)S(1)} %bitcast.664, f32[1,256]{1,0:T(1,128)S(1)} %bitcast.662), channel_id=1, replica_groups=mesh['tm'=8,'env'=4] {'tm'}, use_global_device_ids=true, to_apply=%region_24.25 | all-reduce | flops 768 | bytes 6144 | tf_op jit(solution)/shard_map/pmax | solution.py:135
  317.3 0.6 pad_maximum_fusion.14
  (254 shorter events, 93.9 us)
Async XLA Ops:
  0.6 56.9 %copy-start = (f32[70,256]{1,0:T(8,128)S(1)}, f32[70,256]{1,0:T(8,128)}, u32[]{:S(2)}) copy-start(f32[70,256]{1,0:T(8,128)} %param.23) | copy-start | bytes 215044
  10.2 0.7 copy-start.4
  10.2 0.7 copy-start.5
  10.8 0.7 copy-start.1
  10.8 0.7 copy-start.2
  10.8 0.7 copy-start.3
  11.8 0.8 copy-start.6
  57.6 0.9 copy-start.7
  92.3 0.7 copy-start.8
where the time goes:
time: 318 us
  blocking collectives  187 us (59%)
  matrix products  111 us (35%)
  local copies, waits for them, and re-layouts  9.75 us (3%)
  loops' own time  7.26 us (2%)
    all_gather x4, blocking collectives, sweep(): lax.all_gather(local_shift[None], 'tm', axis=0, tiled=True)  126 us
    dot_general x220, matrix products, exact_dot(): jnp.dot(left, right, precision=lax.Precision.HIGHEST, preferred_element_t...  108 us
    all_gather x1, blocking collectives, body(): all_maps = lax.all_gather(device_map[None], 'tm', axis=0, tiled=True)  31.3 us
    pmax x1, blocking collectives, body(): records.append(lax.pmax(local_max, 'tm'))  21.2 us
    psum x1, blocking collectives, body(): totals = lax.psum(jnp.sum(contact_float, axis=1), 'env')  8.39 us

commit v1 on v0

--- a/solution.py
+++ b/solution.py
@@ -8,6 +8,18 @@
 SUB = 32
 ITERS = 3
 step_length = 0.05
+
+
+def summed_around(value, axis, dim, contribution):
+    count, index, span = (lax.axis_size(axis), lax.axis_index(axis), value.shape[dim])
+    right = [(i, (i + 1) % count) for i in range(count)]
+    held, total = (value, None)
+    for step in range(count):
+        coming = lax.ppermute(held, axis, right) if step < count - 1 else None
+        take_in = contribution(held, (index - step) % count * span)
+        total = take_in if total is None else total + take_in
+        held = coming
+    return total
 
 
 def exact_dot(left, right):
@@ -107,11 +119,16 @@
         local_shift = zero_shift
         for slot_pos in range(local_slices):
             local_shift = exact_dot(step_maps[slot_pos], local_shift) + offsets[slot_pos]
-        entry = lead_state + jnp.einsum(
-            "mij,mje->ie",
-            phi_rows,
-            lax.all_gather(local_shift[None], "tm", axis=0, tiled=True),
-            precision=lax.Precision.HIGHEST,
+        entry = lead_state + summed_around(
+            local_shift[None],
+            "tm",
+            0,
+            lambda own_block, at: jnp.einsum(
+                "mij,mje->ie",
+                lax.dynamic_slice_in_dim(phi_rows, at, own_block.shape[0], axis=0),
+                own_block,
+                precision=lax.Precision.HIGHEST,
+            ),
         )
         start_list = []
         end_list = []

time: 318 us -> 381 us (1.20)
  waiting for transfers between devices: 0 us -> 184 us
  blocking collectives: 187 us -> 56.7 us
  matrix products: 111 us -> 117 us
    ppermute x0 -> x28, waiting for transfers between devices: none -> 184 us  [summed_around(): coming = lax.ppermute(held, axis, right) if step < count - 1 else None]
    all_gather x4 -> x0, blocking collectives: 126 us -> none  [sweep(): lax.all_gather(local_shift[None], 'tm', axis=0, tiled=True)]
    dot_general x4 -> x32, matrix products: 2.69 us -> 8.6 us  [sweep(): jnp.einsum('mij,mje->ie', lax.dynamic_slice_in_dim(phi_rows, at, own_bloc...]
    pmax x1, blocking collectives: 21.2 us -> 17.1 us  [body(): records.append(lax.pmax(local_max, 'tm'))]
  transfers between devices with their start and end apart: 0 -> 28, of which waited for: 0 -> 27; matrix products, arithmetic and copies ran while one was open for 0% -> 4% of each run, Pallas kernels for 0% -> 0%
where the time goes in v1:
time: 381 us; the launch traced here: 380 us
  waiting for transfers between devices  184 us (48%)
  matrix products  117 us (31%)
  blocking collectives  56.7 us (15%)
  local copies, waits for them, and re-layouts  9.48 us (2%)
  loops' own time  7.21 us (2%)
    ppermute x28, waiting for transfers between devices, summed_around(): coming = lax.ppermute(held, axis, right) if step < count - 1 else None  184 us
    dot_general x220, matrix products, exact_dot(): jnp.dot(left, right, precision=lax.Precision.HIGHEST, preferred_element_t...  108 us
    all_gather x1, blocking collectives, body(): all_maps = lax.all_gather(device_map[None], 'tm', axis=0, tiled=True)  31.1 us
    pmax x1, blocking collectives, body(): records.append(lax.pmax(local_max, 'tm'))  17.1 us
    dot_general x32, matrix products, sweep(): jnp.einsum('mij,mje->ie', lax.dynamic_slice_in_dim(phi_rows, at, own_bloc...  8.6 us
    psum x1, blocking collectives, body(): totals = lax.psum(jnp.sum(contact_float, axis=1), 'env')  8.4 us
  transfers between devices with their start and end apart: 28, of which 27 were waited for; matrix products, arithmetic and copies ran while one was open for 4% of the time, Pallas kernels for 0%

profile of v1, /device:TPU:0, one launch (start us, length us, event | category | flops | bytes accessed | tf_op | source)
XLA Modules:
  0.0 380.4 jit_solution(9937002521257712259)
XLA Ops:
  0.6 0.8 convert_reduce_fusion
  1.5 8.4 %psum.7 = f32[4]{0:T(128)S(1)} all-reduce(f32[4]{0:T(128)S(1)} %convert_reduce_fusion), channel_id=1, replica_groups=mesh['tm'=8,'env'=4] {'env'}, use_global_device_ids=true, to_apply=%region_1.0 | all-reduce | flops 4 | bytes 32 | tf_op jit(solution)/shard_map/psum | solution.py:86
  10.4 0.6 copy-done.4
  11.0 0.6 copy-done.1
  14.5 1.5 collective-permute-start
  16.2 0.7 copy-done.8
  17.1 31.1 %all-gather.1 = f32[8,70,70]{2,1,0:T(8,128)S(1)} all-gather(f32[1,70,70]{2,1,0:T(8,128)S(1)} %convolution_bitcast_fusion.1), channel_id=2, replica_groups=mesh['tm'=8,'env'=4] {'tm'}, dimensions={0}, use_global_device_ids=true | all-gather | bytes 176400 | tf_op jit(solution)/shard_map/all_gather | solution.py:104
  48.3 12.9 %while.95 = (s32[]{:T(128)}, f32[70,70]{0,1:T(8,128)S(1)}, f32[8,70,70]{1,2,0:T(8,128)S(1)}, s32[8]{0:T(128)S(1)}, s32[]{:T(128)}, /*index=5*/f32[8,70,70]{2,1,0:T(8,128)S(1)}, s32[]{:T(128)}, s32[]{:T(128)}) while((s32[]{:T(128)}, f32[70,70]{0,1:T(8,128)S(1)}, f32[8,70,70]{1,2,0:T(8,128)S(1)}, s32[8]{0:T(128)S(1)}, s32[]{:T(128)}, ...), condition=%wide.region_3.4_spmd.clone, body=%wide.region_2.3_spmd.clone.sunk | while | flops 4135604 | bytes 206392 | solution.py:115
  48.3 0.7 dynamic_slice.213
  49.9 0.7 dynamic_slice.213
  51.5 0.7 dynamic_slice.213
  53.1 0.7 dynamic_slice.213
  54.7 0.7 dynamic_slice.213
  56.3 0.7 dynamic_slice.213
  57.9 0.7 dynamic_slice.213
  59.5 0.7 dynamic_slice.213
  62.0 0.6 collective-permute-start.1
  62.9 6.2 %collective-permute-done.1 = f32[1,70,256]{2,1,0:T(8,128)S(1)} collective-permute-done((f32[1,70,256]{2,1,0:T(8,128)S(1)}, f32[1,70,256]{2,1,0:T(8,128)S(1)}, u32[]{:S(2)}, u32[]{:S(2)}) %collective-permute-start.1) | collective-permute-done | bytes 71712 | tf_op jit(solution)/shard_map/ppermute | solution.py:18
  69.4 6.8 %collective-permute-done.2 = f32[1,70,256]{2,1,0:T(8,128)S(1)} collective-permute-done((f32[1,70,256]{2,1,0:T(8,128)S(1)}, f32[1,70,256]{2,1,0:T(8,128)S(1)}, u32[]{:S(2)}, u32[]{:S(2)}) %collective-permute-start.2) | collective-permute-done | bytes 71712 | tf_op jit(solution)/shard_map/ppermute | solution.py:18
  76.4 6.8 %collective-permute-done.3 = f32[1,70,256]{2,1,0:T(8,128)S(1)} collective-permute-done((f32[1,70,256]{2,1,0:T(8,128)S(1)}, f32[1,70,256]{2,1,0:T(8,128)S(1)}, u32[]{:S(2)}, u32[]{:S(2)}) %collective-permute-start.3) | collective-permute-done | bytes 71712 | tf_op jit(solution)/shard_map/ppermute | solution.py:18
  83.5 7.5 %collective-permute-done.4 = f32[1,70,256]{2,1,0:T(8,128)S(1)} collective-permute-done((f32[1,70,256]{2,1,0:T(8,128)S(1)}, f32[1,70,256]{2,1,0:T(8,128)S(1)}, u32[]{:S(2)}, u32[]{:S(2)}) %collective-permute-start.4) | collective-permute-done | bytes 71712 | tf_op jit(solution)/shard_map/ppermute | solution.py:18
  91.3 6.8 %collective-permute-done.5 = f32[1,70,256]{2,1,0:T(8,128)S(1)} collective-permute-done((f32[1,70,256]{2,1,0:T(8,128)S(1)}, f32[1,70,256]{2,1,0:T(8,128)S(1)}, u32[]{:S(2)}, u32[]{:S(2)}) %collective-permute-start.5) | collective-permute-done | bytes 71712 | tf_op jit(solution)/shard_map/ppermute | solution.py:18
  98.3 6.8 %collective-permute-done.6 = f32[1,70,256]{2,1,0:T(8,128)S(1)} collective-permute-done((f32[1,70,256]{2,1,0:T(8,128)S(1)}, f32[1,70,256]{2,1,0:T(8,128)S(1)}, u32[]{:S(2)}, u32[]{:S(2)}) %collective-permute-start.6) | collective-permute-done | bytes 71712 | tf_op jit(solution)/shard_map/ppermute | solution.py:18
  105.6 17.2 %while.89 = (s32[]{:T(128)}, f32[2,35,256]{2,1,0:T(8,128)S(1)}, f32[2,35,256]{2,1,0:T(8,128)S(1)}, f32[35]{0:T(128)S(1)}, f32[2,35,256]{2,1,0:T(8,128)S(1)}, /*i...) while((s32[]{:T(128)}, f32[2,35,256]{2,1,0:T(8,128)S(1)}, ...), condition=%wide.region_5.6_spmd, body=%wide.region_4.5_spmd.sunk | while | flops 62504960 | bytes 2680981 | solution.py:64
  106.1 0.5 multiply_add_fusion.107
  107.2 0.5 multiply_add_fusion.108
  110.4 0.5 multiply_add_fusion.107
  111.5 0.5 multiply_add_fusion.108
  119.0 0.5 multiply_add_fusion.107
  120.1 0.5 multiply_add_fusion.108
  122.8 17.2 %while.90 = (s32[]{:T(128)}, f32[2,35,256]{2,1,0:T(8,128)S(1)}, f32[2,35,256]{2,1,0:T(8,128)S(1)}, f32[35]{0:T(128)S(1)}, f32[2,35,256]{2,1,0:T(8,128)S(1)}, /*i...) while((s32[]{:T(128)}, f32[2,35,256]{2,1,0:T(8,128)S(1)}, ...), condition=%wide.region_7.8_spmd, body=%wide.region_6.7_spmd.sunk | while | flops 62504960 | bytes 2680981 | solution.py:64
  141.0 6.8 %collective-permute-done.7 = f32[1,70,256]{2,1,0:T(8,128)S(1)} collective-permute-done((f32[1,70,256]{2,1,0:T(8,128)S(1)}, f32[1,70,256]{2,1,0:T(8,128)S(1)}, u32[]{:S(2)}, u32[]{:S(2)}) %collective-permute-start.7) | collective-permute-done | bytes 71712 | tf_op jit(solution)/shard_map/ppermute | solution.py:18
  148.1 6.8 %collective-permute-done.8 = f32[1,70,256]{2,1,0:T(8,128)S(1)} collective-permute-done((f32[1,70,256]{2,1,0:T(8,128)S(1)}, f32[1,70,256]{2,1,0:T(8,128)S(1)}, u32[]{:S(2)}, u32[]{:S(2)}) %collective-permute-start.8) | collective-permute-done | bytes 71712 | tf_op jit(solution)/shard_map/ppermute | solution.py:18
  155.1 7.2 %collective-permute-done.9 = f32[1,70,256]{2,1,0:T(8,128)S(1)} collective-permute-done((f32[1,70,256]{2,1,0:T(8,128)S(1)}, f32[1,70,256]{2,1,0:T(8,128)S(1)}, u32[]{:S(2)}, u32[]{:S(2)}) %collective-permute-start.9) | collective-permute-done | bytes 71712 | tf_op jit(solution)/shard_map/ppermute | solution.py:18
  162.6 6.8 %collective-permute-done.10 = f32[1,70,256]{2,1,0:T(8,128)S(1)} collective-permute-done((f32[1,70,256]{2,1,0:T(8,128)S(1)}, f32[1,70,256]{2,1,0:T(8,128)S(1)}, u32[]{:S(2)}, u32[]{:S(2)}) %collective-permute-start.10) | collective-permute-done | bytes 71712 | tf_op jit(solution)/shard_map/ppermute | solution.py:18
  169.7 6.8 %collective-permute-done.11 = f32[1,70,256]{2,1,0:T(8,128)S(1)} collective-permute-done((f32[1,70,256]{2,1,0:T(8,128)S(1)}, f32[1,70,256]{2,1,0:T(8,128)S(1)}, u32[]{:S(2)}, u32[]{:S(2)}) %collective-permute-start.11) | collective-permute-done | bytes 71712 | tf_op jit(solution)/shard_map/ppermute | solution.py:18
  176.7 6.8 %collective-permute-done.12 = f32[1,70,256]{2,1,0:T(8,128)S(1)} collective-permute-done((f32[1,70,256]{2,1,0:T(8,128)S(1)}, f32[1,70,256]{2,1,0:T(8,128)S(1)}, u32[]{:S(2)}, u32[]{:S(2)}) %collective-permute-start.12) | collective-permute-done | bytes 71712 | tf_op jit(solution)/shard_map/ppermute | solution.py:18
  183.8 6.8 %collective-permute-done.13 = f32[1,70,256]{2,1,0:T(8,128)S(1)} collective-permute-done((f32[1,70,256]{2,1,0:T(8,128)S(1)}, f32[1,70,256]{2,1,0:T(8,128)S(1)}, u32[]{:S(2)}, u32[]{:S(2)}) %collective-permute-start.13) | collective-permute-done | bytes 71712 | tf_op jit(solution)/shard_map/ppermute | solution.py:18
  191.1 17.2 %while.91 = (s32[]{:T(128)}, f32[2,35,256]{2,1,0:T(8,128)S(1)}, f32[2,35,256]{2,1,0:T(8,128)S(1)}, f32[35]{0:T(128)S(1)}, f32[2,35,256]{2,1,0:T(8,128)S(1)}, /*i...) while((s32[]{:T(128)}, f32[2,35,256]{2,1,0:T(8,128)S(1)}, ...), condition=%wide.region_9.10_spmd, body=%wide.region_8.9_spmd.sunk | while | flops 62504960 | bytes 2680981 | solution.py:64
  191.6 0.5 multiply_add_fusion.115
  192.7 0.5 multiply_add_fusion.116
  204.5 0.5 multiply_add_fusion.115
  205.5 0.5 multiply_add_fusion.116
  208.2 17.2 %while.92 = (s32[]{:T(128)}, f32[2,35,256]{2,1,0:T(8,128)S(1)}, f32[2,35,256]{2,1,0:T(8,128)S(1)}, f32[35]{0:T(128)S(1)}, f32[2,35,256]{2,1,0:T(8,128)S(1)}, /*i...) while((s32[]{:T(128)}, f32[2,35,256]{2,1,0:T(8,128)S(1)}, ...), condition=%wide.region_11.12_spmd, body=%wide.region_10.11_spmd.sunk | while | flops 62504960 | bytes 2680981 | solution.py:64
  226.4 6.8 %collective-permute-done.14 = f32[1,70,256]{2,1,0:T(8,128)S(1)} collective-permute-done((f32[1,70,256]{2,1,0:T(8,128)S(1)}, f32[1,70,256]{2,1,0:T(8,128)S(1)}, u32[]{:S(2)}, u32[]{:S(2)}) %collective-permute-start.14) | collective-permute-done | bytes 71712 | tf_op jit(solution)/shard_map/ppermute | solution.py:18
  233.6 7.2 %collective-permute-done.15 = f32[1,70,256]{2,1,0:T(8,128)S(1)} collective-permute-done((f32[1,70,256]{2,1,0:T(8,128)S(1)}, f32[1,70,256]{2,1,0:T(8,128)S(1)}, u32[]{:S(2)}, u32[]{:S(2)}) %collective-permute-start.15) | collective-permute-done | bytes 71712 | tf_op jit(solution)/shard_map/ppermute | solution.py:18
  241.1 6.8 %collective-permute-done.16 = f32[1,70,256]{2,1,0:T(8,128)S(1)} collective-permute-done((f32[1,70,256]{2,1,0:T(8,128)S(1)}, f32[1,70,256]{2,1,0:T(8,128)S(1)}, u32[]{:S(2)}, u32[]{:S(2)}) %collective-permute-start.16) | collective-permute-done | bytes 71712 | tf_op jit(solution)/shard_map/ppermute | solution.py:18
  248.1 6.8 %collective-permute-done.17 = f32[1,70,256]{2,1,0:T(8,128)S(1)} collective-permute-done((f32[1,70,256]{2,1,0:T(8,128)S(1)}, f32[1,70,256]{2,1,0:T(8,128)S(1)}, u32[]{:S(2)}, u32[]{:S(2)}) %collective-permute-start.17) | collective-permute-done | bytes 71712 | tf_op jit(solution)/shard_map/ppermute | solution.py:18
  255.2 6.8 %collective-permute-done.18 = f32[1,70,256]{2,1,0:T(8,128)S(1)} collective-permute-done((f32[1,70,256]{2,1,0:T(8,128)S(1)}, f32[1,70,256]{2,1,0:T(8,128)S(1)}, u32[]{:S(2)}, u32[]{:S(2)}) %collective-permute-start.18) | collective-permute-done | bytes 71712 | tf_op jit(solution)/shard_map/ppermute | solution.py:18
  262.2 6.8 %collective-permute-done.19 = f32[1,70,256]{2,1,0:T(8,128)S(1)} collective-permute-done((f32[1,70,256]{2,1,0:T(8,128)S(1)}, f32[1,70,256]{2,1,0:T(8,128)S(1)}, u32[]{:S(2)}, u32[]{:S(2)}) %collective-permute-start.19) | collective-permute-done | bytes 71712 | tf_op jit(solution)/shard_map/ppermute | solution.py:18
  269.3 6.8 %collective-permute-done.20 = f32[1,70,256]{2,1,0:T(8,128)S(1)} collective-permute-done((f32[1,70,256]{2,1,0:T(8,128)S(1)}, f32[1,70,256]{2,1,0:T(8,128)S(1)}, u32[]{:S(2)}, u32[]{:S(2)}) %collective-permute-start.20) | collective-permute-done | bytes 71712 | tf_op jit(solution)/shard_map/ppermute | solution.py:18
  276.5 17.2 %while.93 = (s32[]{:T(128)}, f32[2,35,256]{2,1,0:T(8,128)S(1)}, f32[2,35,256]{2,1,0:T(8,128)S(1)}, f32[35]{0:T(128)S(1)}, f32[2,35,256]{2,1,0:T(8,128)S(1)}, /*i...) while((s32[]{:T(128)}, f32[2,35,256]{2,1,0:T(8,128)S(1)}, ...), condition=%wide.region_13.14_spmd, body=%wide.region_12.13_spmd.sunk | while | flops 62504960 | bytes 2680981 | solution.py:64
  282.4 0.5 multiply_add_fusion.124
  293.7 17.1 %while.94 = (s32[]{:T(128)}, f32[2,35,256]{2,1,0:T(8,128)S(1)}, f32[2,35,256]{2,1,0:T(8,128)S(1)}, f32[35]{0:T(128)S(1)}, f32[2,35,256]{2,1,0:T(8,128)S(1)}, /*i...) while((s32[]{:T(128)}, f32[2,35,256]{2,1,0:T(8,128)S(1)}, ...), condition=%wide.region_15.16_spmd, body=%wide.region_14.15_spmd.sunk | while | flops 62504960 | bytes 2680981 | solution.py:64
  311.9 6.8 %collective-permute-done.21 = f32[1,70,256]{2,1,0:T(8,128)S(1)} collective-permute-done((f32[1,70,256]{2,1,0:T(8,128)S(1)}, f32[1,70,256]{2,1,0:T(8,128)S(1)}, u32[]{:S(2)}, u32[]{:S(2)}) %collective-permute-start.21) | collective-permute-done | bytes 71712 | tf_op jit(solution)/shard_map/ppermute | solution.py:18
  319.0 6.8 %collective-permute-done.22 = f32[1,70,256]{2,1,0:T(8,128)S(1)} collective-permute-done((f32[1,70,256]{2,1,0:T(8,128)S(1)}, f32[1,70,256]{2,1,0:T(8,128)S(1)}, u32[]{:S(2)}, u32[]{:S(2)}) %collective-permute-start.22) | collective-permute-done | bytes 71712 | tf_op jit(solution)/shard_map/ppermute | solution.py:18
  326.1 6.8 %collective-permute-done.23 = f32[1,70,256]{2,1,0:T(8,128)S(1)} collective-permute-done((f32[1,70,256]{2,1,0:T(8,128)S(1)}, f32[1,70,256]{2,1,0:T(8,128)S(1)}, u32[]{:S(2)}, u32[]{:S(2)}) %collective-permute-start.23) | collective-permute-done | bytes 71712 | tf_op jit(solution)/shard_map/ppermute | solution.py:18
  333.2 6.8 %collective-permute-done.24 = f32[1,70,256]{2,1,0:T(8,128)S(1)} collective-permute-done((f32[1,70,256]{2,1,0:T(8,128)S(1)}, f32[1,70,256]{2,1,0:T(8,128)S(1)}, u32[]{:S(2)}, u32[]{:S(2)}) %collective-permute-start.24) | collective-permute-done | bytes 71712 | tf_op jit(solution)/shard_map/ppermute | solution.py:18
  340.2 6.8 %collective-permute-done.25 = f32[1,70,256]{2,1,0:T(8,128)S(1)} collective-permute-done((f32[1,70,256]{2,1,0:T(8,128)S(1)}, f32[1,70,256]{2,1,0:T(8,128)S(1)}, u32[]{:S(2)}, u32[]{:S(2)}) %collective-permute-start.25) | collective-permute-done | bytes 71712 | tf_op jit(solution)/shard_map/ppermute | solution.py:18
  347.3 6.8 %collective-permute-done.26 = f32[1,70,256]{2,1,0:T(8,128)S(1)} collective-permute-done((f32[1,70,256]{2,1,0:T(8,128)S(1)}, f32[1,70,256]{2,1,0:T(8,128)S(1)}, u32[]{:S(2)}, u32[]{:S(2)}) %collective-permute-start.26) | collective-permute-done | bytes 71712 | tf_op jit(solution)/shard_map/ppermute | solution.py:18
  354.3 6.8 %collective-permute-done.27 = f32[1,70,256]{2,1,0:T(8,128)S(1)} collective-permute-done((f32[1,70,256]{2,1,0:T(8,128)S(1)}, f32[1,70,256]{2,1,0:T(8,128)S(1)}, u32[]{:S(2)}, u32[]{:S(2)}) %collective-permute-start.27) | collective-permute-done | bytes 71712 | tf_op jit(solution)/shard_map/ppermute | solution.py:18
  361.9 0.7 copy.101
  362.7 17.1 %all-reduce = (f32[1,256]{1,0:T(1,128)S(1)}, f32[1,256]{1,0:T(1,128)S(1)}, f32[1,256]{1,0:T(1,128)S(1)}) all-reduce(f32[1,256]{1,0:T(1,128)S(1)} %bitcast.799, f32[1,256]{1,0:T(1,128)S(1)} %bitcast.800, f32[1,256]{1,0:T(1,128)S(1)} %bitcast.798), channel_id=1, replica_groups=mesh['tm'=8,'env'=4] {'tm'}, use_global_device_ids=true, to_apply=%region_24.25 | all-reduce | flops 768 | bytes 6144 | tf_op jit(solution)/shard_map/pmax | solution.py:152
  379.8 0.6 pad_maximum_fusion.14
  (334 shorter events, 113.6 us)
Async XLA Ops:
  0.6 60.5 %copy-start = (f32[70,256]{1,0:T(8,128)S(1)}, f32[70,256]{1,0:T(8,128)}, u32[]{:S(2)}) copy-start(f32[70,256]{1,0:T(8,128)} %param.23) | copy-start | bytes 215044
  10.3 0.7 copy-start.4
  10.3 0.7 copy-start.5
  10.3 1.4 copy-start.6
  11.0 0.7 copy-start.1
  11.0 0.7 copy-start.2
  11.0 0.7 copy-start.3
  12.4 0.9 copy-start.7
  14.5 47.5 %collective-permute-start = (f32[1,70,256]{2,1,0:T(8,128)S(1)}, f32[1,70,256]{2,1,0:T(8,128)S(1)}, u32[]{:S(2)}, u32[]{:S(2)}) collective-permute-start(f32[1,70,256]{2,1,0:T(8,128)S(1)} %bitcast.793), channel_id=1, source_target_pairs={{0,4},{4,8},{8,12},{12,16},{16,20},{20,24},{24,28},{28,0},{1,5},{5... | collective-permute-start | bytes 215048 | tf_op jit(solution)/shard_map/ppermute | solution.py:18
  16.2 0.7 copy-start.8
  62.0 7.1 %collective-permute-start.1 = (f32[1,70,256]{2,1,0:T(8,128)S(1)}, f32[1,70,256]{2,1,0:T(8,128)S(1)}, u32[]{:S(2)}, u32[]{:S(2)}) collective-permute-start(f32[1,70,256]{2,1,0:T(8,128)S(1)} %collective-permute-done), channel_id=1, source_target_pairs={{0,4},{4,8},{8,12},{12,16},{16,20},{20,24},{24,28},{28,0},{1,5},{5... | collective-permute-start | bytes 215048 | tf_op jit(solution)/shard_map/ppermute | solution.py:18
  69.1 7.0 %collective-permute-start.2 = (f32[1,70,256]{2,1,0:T(8,128)S(1)}, f32[1,70,256]{2,1,0:T(8,128)S(1)}, u32[]{:S(2)}, u32[]{:S(2)}) collective-permute-start(f32[1,70,256]{2,1,0:T(8,128)S(1)} %collective-permute-done.1), channel_id=1, source_target_pairs={{0,4},{4,8},{8,12},{12,16},{16,20},{20,24},{24,28},{28,0},{1,5},{5... | collective-permute-start | bytes 215048 | tf_op jit(solution)/shard_map/ppermute | solution.py:18
  76.2 7.0 %collective-permute-start.3 = (f32[1,70,256]{2,1,0:T(8,128)S(1)}, f32[1,70,256]{2,1,0:T(8,128)S(1)}, u32[]{:S(2)}, u32[]{:S(2)}) collective-permute-start(f32[1,70,256]{2,1,0:T(8,128)S(1)} %collective-permute-done.2), channel_id=1, source_target_pairs={{0,4},{4,8},{8,12},{12,16},{16,20},{20,24},{24,28},{28,0},{1,5},{5... | collective-permute-start | bytes 215048 | tf_op jit(solution)/shard_map/ppermute | solution.py:18
  83.2 7.8 %collective-permute-start.4 = (f32[1,70,256]{2,1,0:T(8,128)S(1)}, f32[1,70,256]{2,1,0:T(8,128)S(1)}, u32[]{:S(2)}, u32[]{:S(2)}) collective-permute-start(f32[1,70,256]{2,1,0:T(8,128)S(1)} %collective-permute-done.3), channel_id=1, source_target_pairs={{0,4},{4,8},{8,12},{12,16},{16,20},{20,24},{24,28},{28,0},{1,5},{5... | collective-permute-start | bytes 215048 | tf_op jit(solution)/shard_map/ppermute | solution.py:18
  91.0 7.0 %collective-permute-start.5 = (f32[1,70,256]{2,1,0:T(8,128)S(1)}, f32[1,70,256]{2,1,0:T(8,128)S(1)}, u32[]{:S(2)}, u32[]{:S(2)}) collective-permute-start(f32[1,70,256]{2,1,0:T(8,128)S(1)} %collective-permute-done.4), channel_id=1, source_target_pairs={{0,4},{4,8},{8,12},{12,16},{16,20},{20,24},{24,28},{28,0},{1,5},{5... | collective-permute-start | bytes 215048 | tf_op jit(solution)/shard_map/ppermute | solution.py:18
  98.0 7.1 %collective-permute-start.6 = (f32[1,70,256]{2,1,0:T(8,128)S(1)}, f32[1,70,256]{2,1,0:T(8,128)S(1)}, u32[]{:S(2)}, u32[]{:S(2)}) collective-permute-start(f32[1,70,256]{2,1,0:T(8,128)S(1)} %collective-permute-done.5), channel_id=1, source_target_pairs={{0,4},{4,8},{8,12},{12,16},{16,20},{20,24},{24,28},{28,0},{1,5},{5... | collective-permute-start | bytes 215048 | tf_op jit(solution)/shard_map/ppermute | solution.py:18
  140.7 7.1 %collective-permute-start.7 = (f32[1,70,256]{2,1,0:T(8,128)S(1)}, f32[1,70,256]{2,1,0:T(8,128)S(1)}, u32[]{:S(2)}, u32[]{:S(2)}) collective-permute-start(f32[1,70,256]{2,1,0:T(8,128)S(1)} %bitcast.795), channel_id=1, source_target_pairs={{0,4},{4,8},{8,12},{12,16},{16,20},{20,24},{24,28},{28,0},{1,5},{5... | collective-permute-start | bytes 215048 | tf_op jit(solution)/shard_map/ppermute | solution.py:18
  147.8 7.0 %collective-permute-start.8 = (f32[1,70,256]{2,1,0:T(8,128)S(1)}, f32[1,70,256]{2,1,0:T(8,128)S(1)}, u32[]{:S(2)}, u32[]{:S(2)}) collective-permute-start(f32[1,70,256]{2,1,0:T(8,128)S(1)} %collective-permute-done.7), channel_id=1, source_target_pairs={{0,4},{4,8},{8,12},{12,16},{16,20},{20,24},{24,28},{28,0},{1,5},{5... | collective-permute-start | bytes 215048 | tf_op jit(solution)/shard_map/ppermute | solution.py:18
  154.9 7.5 %collective-permute-start.9 = (f32[1,70,256]{2,1,0:T(8,128)S(1)}, f32[1,70,256]{2,1,0:T(8,128)S(1)}, u32[]{:S(2)}, u32[]{:S(2)}) collective-permute-start(f32[1,70,256]{2,1,0:T(8,128)S(1)} %collective-permute-done.8), channel_id=1, source_target_pairs={{0,4},{4,8},{8,12},{12,16},{16,20},{20,24},{24,28},{28,0},{1,5},{5... | collective-permute-start | bytes 215048 | tf_op jit(solution)/shard_map/ppermute | solution.py:18
  162.3 7.1 %collective-permute-start.10 = (f32[1,70,256]{2,1,0:T(8,128)S(1)}, f32[1,70,256]{2,1,0:T(8,128)S(1)}, u32[]{:S(2)}, u32[]{:S(2)}) collective-permute-start(f32[1,70,256]{2,1,0:T(8,128)S(1)} %collective-permute-done.9), channel_id=1, source_target_pairs={{0,4},{4,8},{8,12},{12,16},{16,20},{20,24},{24,28},{28,0},{1,5},{5... | collective-permute-start | bytes 215048 | tf_op jit(solution)/shard_map/ppermute | solution.py:18
  169.4 7.0 %collective-permute-start.11 = (f32[1,70,256]{2,1,0:T(8,128)S(1)}, f32[1,70,256]{2,1,0:T(8,128)S(1)}, u32[]{:S(2)}, u32[]{:S(2)}) collective-permute-start(f32[1,70,256]{2,1,0:T(8,128)S(1)} %collective-permute-done.10), channel_id=1, source_target_pairs={{0,4},{4,8},{8,12},{12,16},{16,20},{20,24},{24,28},{28,0},{1,5},{5... | collective-permute-start | bytes 215048 | tf_op jit(solution)/shard_map/ppermute | solution.py:18
  176.4 7.0 %collective-permute-start.12 = (f32[1,70,256]{2,1,0:T(8,128)S(1)}, f32[1,70,256]{2,1,0:T(8,128)S(1)}, u32[]{:S(2)}, u32[]{:S(2)}) collective-permute-start(f32[1,70,256]{2,1,0:T(8,128)S(1)} %collective-permute-done.11), channel_id=1, source_target_pairs={{0,4},{4,8},{8,12},{12,16},{16,20},{20,24},{24,28},{28,0},{1,5},{5... | collective-permute-start | bytes 215048 | tf_op jit(solution)/shard_map/ppermute | solution.py:18
  183.5 7.1 %collective-permute-start.13 = (f32[1,70,256]{2,1,0:T(8,128)S(1)}, f32[1,70,256]{2,1,0:T(8,128)S(1)}, u32[]{:S(2)}, u32[]{:S(2)}) collective-permute-start(f32[1,70,256]{2,1,0:T(8,128)S(1)} %collective-permute-done.12), channel_id=1, source_target_pairs={{0,4},{4,8},{8,12},{12,16},{16,20},{20,24},{24,28},{28,0},{1,5},{5... | collective-permute-start | bytes 215048 | tf_op jit(solution)/shard_map/ppermute | solution.py:18
  226.2 7.1 %collective-permute-start.14 = (f32[1,70,256]{2,1,0:T(8,128)S(1)}, f32[1,70,256]{2,1,0:T(8,128)S(1)}, u32[]{:S(2)}, u32[]{:S(2)}) collective-permute-start(f32[1,70,256]{2,1,0:T(8,128)S(1)} %bitcast.796), channel_id=1, source_target_pairs={{0,4},{4,8},{8,12},{12,16},{16,20},{20,24},{24,28},{28,0},{1,5},{5... | collective-permute-start | bytes 215048 | tf_op jit(solution)/shard_map/ppermute | solution.py:18
  233.3 7.5 %collective-permute-start.15 = (f32[1,70,256]{2,1,0:T(8,128)S(1)}, f32[1,70,256]{2,1,0:T(8,128)S(1)}, u32[]{:S(2)}, u32[]{:S(2)}) collective-permute-start(f32[1,70,256]{2,1,0:T(8,128)S(1)} %collective-permute-done.14), channel_id=1, source_target_pairs={{0,4},{4,8},{8,12},{12,16},{16,20},{20,24},{24,28},{28,0},{1,5},{5... | collective-permute-start | bytes 215048 | tf_op jit(solution)/shard_map/ppermute | solution.py:18
  240.8 7.0 %collective-permute-start.16 = (f32[1,70,256]{2,1,0:T(8,128)S(1)}, f32[1,70,256]{2,1,0:T(8,128)S(1)}, u32[]{:S(2)}, u32[]{:S(2)}) collective-permute-start(f32[1,70,256]{2,1,0:T(8,128)S(1)} %collective-permute-done.15), channel_id=1, source_target_pairs={{0,4},{4,8},{8,12},{12,16},{16,20},{20,24},{24,28},{28,0},{1,5},{5... | collective-permute-start | bytes 215048 | tf_op jit(solution)/shard_map/ppermute | solution.py:18
  247.8 7.0 %collective-permute-start.17 = (f32[1,70,256]{2,1,0:T(8,128)S(1)}, f32[1,70,256]{2,1,0:T(8,128)S(1)}, u32[]{:S(2)}, u32[]{:S(2)}) collective-permute-start(f32[1,70,256]{2,1,0:T(8,128)S(1)} %collective-permute-done.16), channel_id=1, source_target_pairs={{0,4},{4,8},{8,12},{12,16},{16,20},{20,24},{24,28},{28,0},{1,5},{5... | collective-permute-start | bytes 215048 | tf_op jit(solution)/shard_map/ppermute | solution.py:18
  254.9 7.0 %collective-permute-start.18 = (f32[1,70,256]{2,1,0:T(8,128)S(1)}, f32[1,70,256]{2,1,0:T(8,128)S(1)}, u32[]{:S(2)}, u32[]{:S(2)}) collective-permute-start(f32[1,70,256]{2,1,0:T(8,128)S(1)} %collective-permute-done.17), channel_id=1, source_target_pairs={{0,4},{4,8},{8,12},{12,16},{16,20},{20,24},{24,28},{28,0},{1,5},{5... | collective-permute-start | bytes 215048 | tf_op jit(solution)/shard_map/ppermute | solution.py:18
  261.9 7.0 %collective-permute-start.19 = (f32[1,70,256]{2,1,0:T(8,128)S(1)}, f32[1,70,256]{2,1,0:T(8,128)S(1)}, u32[]{:S(2)}, u32[]{:S(2)}) collective-permute-start(f32[1,70,256]{2,1,0:T(8,128)S(1)} %collective-permute-done.18), channel_id=1, source_target_pairs={{0,4},{4,8},{8,12},{12,16},{16,20},{20,24},{24,28},{28,0},{1,5},{5... | collective-permute-start | bytes 215048 | tf_op jit(solution)/shard_map/ppermute | solution.py:18
  269.0 7.1 %collective-permute-start.20 = (f32[1,70,256]{2,1,0:T(8,128)S(1)}, f32[1,70,256]{2,1,0:T(8,128)S(1)}, u32[]{:S(2)}, u32[]{:S(2)}) collective-permute-start(f32[1,70,256]{2,1,0:T(8,128)S(1)} %collective-permute-done.19), channel_id=1, source_target_pairs={{0,4},{4,8},{8,12},{12,16},{16,20},{20,24},{24,28},{28,0},{1,5},{5... | collective-permute-start | bytes 215048 | tf_op jit(solution)/shard_map/ppermute | solution.py:18
  311.6 7.1 %collective-permute-start.21 = (f32[1,70,256]{2,1,0:T(8,128)S(1)}, f32[1,70,256]{2,1,0:T(8,128)S(1)}, u32[]{:S(2)}, u32[]{:S(2)}) collective-permute-start(f32[1,70,256]{2,1,0:T(8,128)S(1)} %bitcast.794), channel_id=1, source_target_pairs={{0,4},{4,8},{8,12},{12,16},{16,20},{20,24},{24,28},{28,0},{1,5},{5... | collective-permute-start | bytes 215048 | tf_op jit(solution)/shard_map/ppermute | solution.py:18
  318.8 7.0 %collective-permute-start.22 = (f32[1,70,256]{2,1,0:T(8,128)S(1)}, f32[1,70,256]{2,1,0:T(8,128)S(1)}, u32[]{:S(2)}, u32[]{:S(2)}) collective-permute-start(f32[1,70,256]{2,1,0:T(8,128)S(1)} %collective-permute-done.21), channel_id=1, source_target_pairs={{0,4},{4,8},{8,12},{12,16},{16,20},{20,24},{24,28},{28,0},{1,5},{5... | collective-permute-start | bytes 215048 | tf_op jit(solution)/shard_map/ppermute | solution.py:18
  325.8 7.1 %collective-permute-start.23 = (f32[1,70,256]{2,1,0:T(8,128)S(1)}, f32[1,70,256]{2,1,0:T(8,128)S(1)}, u32[]{:S(2)}, u32[]{:S(2)}) collective-permute-start(f32[1,70,256]{2,1,0:T(8,128)S(1)} %collective-permute-done.22), channel_id=1, source_target_pairs={{0,4},{4,8},{8,12},{12,16},{16,20},{20,24},{24,28},{28,0},{1,5},{5... | collective-permute-start | bytes 215048 | tf_op jit(solution)/shard_map/ppermute | solution.py:18
  332.9 7.0 %collective-permute-start.24 = (f32[1,70,256]{2,1,0:T(8,128)S(1)}, f32[1,70,256]{2,1,0:T(8,128)S(1)}, u32[]{:S(2)}, u32[]{:S(2)}) collective-permute-start(f32[1,70,256]{2,1,0:T(8,128)S(1)} %collective-permute-done.23), channel_id=1, source_target_pairs={{0,4},{4,8},{8,12},{12,16},{16,20},{20,24},{24,28},{28,0},{1,5},{5... | collective-permute-start | bytes 215048 | tf_op jit(solution)/shard_map/ppermute | solution.py:18
  339.9 7.0 %collective-permute-start.25 = (f32[1,70,256]{2,1,0:T(8,128)S(1)}, f32[1,70,256]{2,1,0:T(8,128)S(1)}, u32[]{:S(2)}, u32[]{:S(2)}) collective-permute-start(f32[1,70,256]{2,1,0:T(8,128)S(1)} %collective-permute-done.24), channel_id=1, source_target_pairs={{0,4},{4,8},{8,12},{12,16},{16,20},{20,24},{24,28},{28,0},{1,5},{5... | collective-permute-start | bytes 215048 | tf_op jit(solution)/shard_map/ppermute | solution.py:18
  347.0 7.0 %collective-permute-start.26 = (f32[1,70,256]{2,1,0:T(8,128)S(1)}, f32[1,70,256]{2,1,0:T(8,128)S(1)}, u32[]{:S(2)}, u32[]{:S(2)}) collective-permute-start(f32[1,70,256]{2,1,0:T(8,128)S(1)} %collective-permute-done.25), channel_id=1, source_target_pairs={{0,4},{4,8},{8,12},{12,16},{16,20},{20,24},{24,28},{28,0},{1,5},{5... | collective-permute-start | bytes 215048 | tf_op jit(solution)/shard_map/ppermute | solution.py:18
  354.1 7.0 %collective-permute-start.27 = (f32[1,70,256]{2,1,0:T(8,128)S(1)}, f32[1,70,256]{2,1,0:T(8,128)S(1)}, u32[]{:S(2)}, u32[]{:S(2)}) collective-permute-start(f32[1,70,256]{2,1,0:T(8,128)S(1)} %collective-permute-done.26), channel_id=1, source_target_pairs={{0,4},{4,8},{8,12},{12,16},{16,20},{20,24},{24,28},{28,0},{1,5},{5... | collective-permute-start | bytes 215048 | tf_op jit(solution)/shard_map/ppermute | solution.py:18
